TPU v7x, 32 devices: a whole 2x2x4 slice. The times are simulated.
32 devices in a mesh: tok: 8 (over y, x, core), exp: 4 (over z).
Axes of the slice: x: 2, y: 2, z: 4, core: 2. Of those that a mesh axis runs over, the one named last changes fastest.
Arguments:
- expert_rows: bfloat16 [4, 2048, 4096], P('exp', 'tok'), may hold values from -480 to 480
- router_input: bfloat16 [2048, 4096], P(('tok', 'exp')), may hold values from -6 to 6
- router_weight: float32 [4096, 4], replicated, may hold values from -0.09375 to 0.09375
- assign: int32 [2048, 2], P(('tok', 'exp')), may hold values from 0 to 3, all different within a row
- targets: int32 [2048], P(('tok', 'exp')), may hold values from 0 to 15999
- head: bfloat16 [4096, 16000], P('tok', 'exp'), may hold values from -0.35 to 0.35
Outputs:
- token_loss: float32 [2048], P(('tok', 'exp'))
- router_grad: float32 [4096, 4], replicated
- mean_loss: float32 [], replicated
All inputs are finite; a program needn't handle non-finite values.
Results may differ from a plain program's by a relative error of at most 0.007.
Values may be sent and summed in bfloat16 or wider, within the bound.
A program may use at most 128 MiB of HBM per device.

v0:
```python
import math
import jax
import jax.numpy as jnp
from jax import lax
from jax.sharding import PartitionSpec as P


def shards(expert_rows, router_input, router_weight, assign, targets, head):
    experts = router_weight.shape[1]
    own_rows = router_input.shape[0]
    tokens_all = own_rows * lax.axis_size("tok") * lax.axis_size("exp")
    loss_scale = 1.0 / math.sqrt(tokens_all)
    inputs = router_input.astype(jnp.float32)
    gate_logits = jnp.dot(inputs, router_weight, precision=lax.Precision.HIGHEST)
    labels = jnp.arange(experts, dtype=jnp.int32)
    first_hot = (assign[:, 0:1] == labels[None, :]).astype(jnp.float32)
    second_hot = (assign[:, 1:2] == labels[None, :]).astype(jnp.float32)
    differ = first_hot - second_hot
    mix_share = jax.nn.sigmoid(jnp.sum(gate_logits * differ, axis=1))
    mixing = mix_share[:, None] * first_hot + (1.0 - mix_share)[:, None] * second_hot
    local_rows = lax.all_to_all(expert_rows, "exp", split_axis=1, concat_axis=0, tiled=True)
    local_wide = local_rows.astype(jnp.float32)
    mixed_own = jnp.sum(mixing.T[:, :, None] * local_wide, axis=0).astype(jnp.bfloat16)
    mixed_rows, group_targets = (
        lax.all_gather(mixed_own, "exp", axis=0, tiled=True),
        lax.all_gather(targets, "exp", axis=0, tiled=True),
    )
    shard_width = head.shape[1]
    full_head = lax.all_gather(head, "tok", axis=0, tiled=True)
    logits = jnp.dot(mixed_rows, full_head, preferred_element_type=jnp.float32)
    first_col = lax.axis_index("exp") * shard_width
    columns = first_col + jnp.arange(shard_width, dtype=jnp.int32)
    target_hit = group_targets[:, None] == columns[None, :]
    picked = jnp.sum(jnp.where(target_hit, logits, 0.0), axis=1)
    local_top = jnp.max(logits, axis=1)
    row_top = lax.pmax(local_top, "exp")
    exp_total, target_logit = lax.psum(
        (jnp.sum(jnp.exp(logits - row_top[:, None]), axis=1), picked), "exp"
    )
    log_total = row_top + jnp.log(exp_total)
    group_loss = log_total - target_logit
    own_loss = lax.dynamic_slice_in_dim(group_loss, lax.axis_index("exp") * own_rows, own_rows, 0)
    loss_sum = lax.psum(jnp.sum(own_loss), ("tok", "exp"))
    slope = (
        loss_scale * (jnp.exp(logits - log_total[:, None]) - target_hit.astype(jnp.float32))
    ).astype(jnp.bfloat16)
    hidden_slope = lax.psum_scatter(
        lax.dot_general(
            slope, full_head, (((1,), (1,)), ((), ())), preferred_element_type=jnp.float32
        ).astype(jnp.bfloat16),
        "exp",
        scatter_dimension=0,
        tiled=True,
    ).astype(jnp.float32)
    weight_slope = jnp.sum(hidden_slope[None, :, :] * local_wide, axis=2).T
    spread = jnp.sum(weight_slope * differ, axis=1) * mix_share * (1.0 - mix_share)
    gate_slope = spread[:, None] * differ
    router_part = jnp.dot(inputs.T, gate_slope, precision=lax.Precision.HIGHEST)
    router_sum = lax.psum(router_part, ("tok", "exp"))
    mean_loss = loss_sum / tokens_all
    return (own_loss, router_sum, mean_loss)


def solution(mesh):
    in_specs = (
        P("exp", "tok", None),
        P(("tok", "exp"), None),
        P(),
        P(("tok", "exp"), None),
        P(("tok", "exp")),
        P("tok", "exp"),
    )
    out_specs = (P(("tok", "exp")), P(), P())
    return jax.shard_map(shards, mesh=mesh, in_specs=in_specs, out_specs=out_specs, check_vma=False)
```

profile of v0, /device:TPU:1, one launch (start us, length us, event | category | flops | bytes accessed | tf_op | source)
XLA Modules:
  0.0 542.0 jit_solution(5459968139769704115)
XLA Ops:
  7.2 0.0 copy-start
  7.2 8.4 %copy.16 = bf16[1,256,4096]{2,0,1:T(2,128)(2,1)} copy(bf16[1,256,4096]{2,1,0:T(8,128)(2,1)} %param.6) | data formatting | bytes 4194304 | tf_op args[0]
  15.6 0.5 broadcast.107
  16.1 13.5 %reduce.1 = bf16[256,4096]{1,0:T(8,128)(2,1)S(1)} reduce(bf16[256,1,4096]{2,1,0:T(2,128)(2,1)} %bitcast.29, bf16[]{:T(256)} %broadcast.107), dimensions={1}, to_apply=%bitcast.25.reduce_sub_computation | reduce | bytes 4194306
  29.6 0.0 copy-start.3
  29.6 0.0 copy-start.2
  29.6 2.8 reshape.110
  32.4 5.4 all-to-all-start
  37.8 0.0 all-gather.3.cloned.1.call-start
  37.8 0.0 copy-done.3
  37.8 0.0 copy-done
  37.8 0.0 copy-done.2
  37.9 0.5 fusion.10
  38.4 47.2 %all-to-all-done = bf16[4,2,131072]{2,1,0:T(2,128)(2,1)S(1)} async-done(((bf16[4,2,131072]{2,1,0:T(2,128)(2,1)}), bf16[4,2,131072]{2,1,0:T(2,128)(2,1)S(1)}, u32[]{:S(2)}, u32[]{:S(2)}) %all-to-all-start) | async-done | bytes 2097184 | tf_op jit(solution)/shard_map/all_to_all | solution.py:21
  85.6 3.3 reshape.111
  88.9 6.0 %copy_convert_fusion = f32[1,256,4096]{2,1,0:T(8,128)S(1)} fusion(bf16[1,256,4096]{2,0,1:T(2,128)(2,1)} %bitcast.27), kind=kLoop, calls=%fused_computation.12 | loop fusion | flops 1048576 | bytes 6291456 | tf_op jit(solution)/shard_map/convert_element_type | solution.py:22
  94.9 0.0 copy-start.5
  94.9 0.0 copy-start.4
  94.9 1.4 multiply_reduce_fusion
  96.3 0.0 all-gather.3.cloned.1.call-update
  96.3 0.0 all-gather.5.cloned.1.call-start
  96.3 0.7 all-gather.5.cloned.1.call-update
  97.1 0.2 reduce-scatter.2.cloned.1.call-start
  97.3 0.0 copy-done.5
  97.3 0.6 dynamic-slice
  98.5 0.0 copy-done.4
  98.6 0.2 dynamic-update-slice
  98.8 4.0 all-reduce
  102.8 39.0 %all-gather.3.cloned.1.call-done = bf16[256,4096]{1,0:T(8,128)(2,1)} async-done(((bf16[64,4096]{1,0:T(8,128)(2,1)}), bf16[256,4096]{1,0:T(8,128)(2,1)}) %all-gather.3.cloned.1.call-update) | async-done | bytes 2097168 | tf_op jit(solution)/shard_map/all_gather | solution.py:25
  141.8 165.1 %all-gather.5.cloned.1.call-done = bf16[4096,4000]{0,1:T(8,128)(2,1)} async-done(((bf16[512,4000]{0,1:T(8,128)(2,1)}), bf16[4096,4000]{0,1:T(8,128)(2,1)}) %all-gather.5.cloned.1.call-update) | async-done | bytes 32768016 | tf_op jit(solution)/shard_map/all_gather | solution.py:29
  306.9 16.2 %fusion.19 = (f32[256]{0:T(256)S(1)}, f32[256,4000]{0,1:T(8,128)}) fusion(bf16[256,4096]{1,0:T(8,128)(2,1)} %all-gather.3.cloned.1.call-done, bf16[4096,4000]{0,1:T(8,128)(2,1)} %all-gather.5.cloned.1.call-done), kind=kOutput, calls=%fused_computation.41 | convolution fusion | flops 8389632000 | bytes 38962176 | tf_op jit(solution)/shard_map/dot_general | solution.py:30
  323.2 9.7 %pmax.7 = f32[256]{0:T(256)S(1)} all-reduce(f32[256]{0:T(256)S(1)} %get-tuple-element.15), channel_id=1, replica_groups=mesh['tok'=8,'exp'=4] {'exp'}, use_global_device_ids=true, to_apply=%region_3.4 | all-reduce | flops 256 | bytes 2048 | tf_op jit(solution)/shard_map/pmax | solution.py:36
  332.8 3.9 fusion.1
  336.7 6.6 %all-reduce.1 = (f32[256]{0:T(256)S(1)}, f32[256]{0:T(256)S(1)}) all-reduce(f32[256]{0:T(256)S(1)} %get-tuple-element.4, f32[256]{0:T(256)S(1)} %get-tuple-element.3), channel_id=1, replica_groups=mesh['tok'=8,'exp'=4] {'exp'}, use_global_device_ids=true, to_apply=%region_5.6 | all-reduce | flops 512 | bytes 4096 | tf_op jit(solution)/shard_map/psum | solution.py:37
  343.3 17.2 %convolution_convert_fusion = bf16[256,4096]{1,0:T(8,128)(2,1)} fusion(bf16[4096,4000]{0,1:T(8,128)(2,1)} %all-gather.5.cloned.1.call-done, f32[256,4000]{0,1:T(8,128)} %get-tuple-element.16, f32[256]{0:T(256)S(1)} %get-tuple-element.10, s32[256]{0:T(256)S(1)} %all-reduce, s32[4000]{0:T(1024)S(1)} %iota_add_fusion), kind=kOutput, calls=%fused_computation | convolution fusion | flops 8395800576 | bytes 38979200 | tf_op jit(solution)/shard_map/dot_general | solution.py:48
  360.5 0.0 reduce-scatter.2.cloned.1.call-update
  360.5 0.0 all-reduce.4.cloned.1.call-start
  360.6 45.4 %reduce-scatter.2.cloned.1.call-done = bf16[64,4096]{1,0:T(8,128)(2,1)} async-done(((bf16[256,4096]{1,0:T(8,128)(2,1)}), bf16[64,4096]{1,0:T(8,128)(2,1)}) %reduce-scatter.2.cloned.1.call-update) | async-done | bytes 524304 | tf_op jit(solution)/shard_map/reduce_scatter | solution.py:47
  406.0 1.7 mul.89
  407.6 0.7 copy-done.1
  408.3 2.4 fusion
  410.7 0.1 reduce_sum.70
  410.8 1.0 convolution_bitcast_fusion
  411.8 0.0 all-reduce.4.cloned.1.call-update
  411.8 1.2 fusion.17
  413.0 39.8 %psum.31 = f32[]{:T(128)} all-reduce(f32[]{:T(128)} %get-tuple-element.7), channel_id=1, replica_groups=mesh['tok'=8,'exp'=4] {'tok','exp'}, use_global_device_ids=true, to_apply=%region_13.14 | all-reduce | flops 1 | bytes 8 | tf_op jit(solution)/shard_map/psum | solution.py:43
  453.4 79.5 %all-reduce.4.cloned.1.call-done = f32[4096,4]{0,1:T(4,128)} async-done(((f32[4096,4]{0,1:T(4,128)}), f32[4096,4]{0,1:T(4,128)}) %all-reduce.4.cloned.1.call-update) | async-done | bytes 65552 | tf_op jit(solution)/shard_map/psum | solution.py:59
  532.9 1.5 copy.19
  (9 shorter events, 0.1 us)
Async XLA Ops:
  7.2 30.7 %copy-start = (bf16[64,4096]{1,0:T(8,128)(2,1)S(1)}, bf16[64,4096]{1,0:T(8,128)(2,1)}, u32[]{:S(2)}) copy-start(bf16[64,4096]{1,0:T(8,128)(2,1)} %param.7) | copy-start | bytes 1572868
  29.6 8.2 %copy-start.3 = (s32[64,2]{0,1:T(2,128)S(1)}, s32[64,2]{0,1:T(2,128)}, u32[]{:S(2)}) copy-start(s32[64,2]{0,1:T(2,128)} %param.9) | copy-start | bytes 1540
  29.6 8.2 %copy-start.2 = (f32[4096,4]{0,1:T(4,128)S(1)}, f32[4096,4]{0,1:T(4,128)}, u32[]{:S(2)}) copy-start(f32[4096,4]{0,1:T(4,128)} %param.8) | copy-start | bytes 196612
  32.4 53.2 %all-to-all-start = ((bf16[4,2,131072]{2,1,0:T(2,128)(2,1)}), bf16[4,2,131072]{2,1,0:T(2,128)(2,1)S(1)}, u32[]{:S(2)}, u32[]{:S(2)}) async-start(bf16[4,2,131072]{2,1,0:T(2,128)(2,1)} %reshape.110), calls=%async_computation | async-start | bytes 4194304 | tf_op jit(solution)/shard_map/all_to_all | solution.py:21
  37.8 104.0 %all-gather.3.cloned.1.call-start = ((), (), s32[]{:S(2)}) async-start(), calls=%async_computation.2 | async-start | bytes 2621440 | tf_op jit(solution)/shard_map/all_gather | solution.py:25
  94.9 2.4 copy-start.5
  94.9 3.6 copy-start.4
  96.3 210.6 %all-gather.5.cloned.1.call-start = ((), (), s32[]{:S(2)}) async-start(), calls=%async_computation.3 | async-start | bytes 36864000 | tf_op jit(solution)/shard_map/all_gather | solution.py:29
  97.1 308.9 %reduce-scatter.2.cloned.1.call-start = ((), (), s32[]{:S(2)}) async-start(), calls=%async_computation.4 | async-start | bytes 2621440 | tf_op jit(solution)/shard_map/reduce_scatter | solution.py:47
  360.5 172.3 %all-reduce.4.cloned.1.call-start = ((), (), s32[]{:S(2)}) async-start(), calls=%async_computation.5 | async-start | bytes 131072 | tf_op jit(solution)/shard_map/psum | solution.py:59
  406.0 2.3 copy-start.1
Sparse Core Ops, SparseCore 0:
  96.4 45.3 all-gather.2
  143.6 163.2 all-gather.4
  360.7 45.2 reduce-scatter.1
  412.0 120.8 all-reduce.3
where the time goes:
time: 543 us; the launch traced here: 542 us
  waiting for transfers between devices  377 us (69%)
  blocking collectives  60.1 us (11%)
  matrix products  34.9 us (6%)
  other arithmetic  28.4 us (5%)
  local copies, waits for them, and re-layouts  19.7 us (4%)
  between operations  16.3 us (3%)
  starting transfers between devices  5.71 us (1%)
    all_gather x1, waiting for transfers between devices, shards(): full_head = lax.all_gather(head, 'tok', axis=0, tiled=True)  165 us
    psum x1, waiting for transfers between devices, shards(): router_sum = lax.psum(router_part, ('tok', 'exp'))  79.5 us
    all_to_all x1, waiting for transfers between devices, shards(): lax.all_to_all(expert_rows, 'exp', split_axis=1, concat_axis=0, tiled=True)  47.2 us
    reduce_scatter x1, waiting for transfers between devices, shards(): lax.psum_scatter(lax.dot_general(slope, full_head, (((1,), (1,)), ((), ()...  45.4 us
    psum x1, blocking collectives, shards(): loss_sum = lax.psum(jnp.sum(own_loss), ('tok', 'exp'))  39.8 us
    all_gather x1, waiting for transfers between devices, shards(): lax.all_gather(mixed_own, 'exp', axis=0, tiled=True)  39 us
    unnamed x20, local copies, waits for them, and re-layouts  18 us
    dot_general x1, matrix products, shards(): lax.dot_general(slope, full_head, (((1,), (1,)), ((), ())), preferred_ele...  17.2 us
  transfers between devices with their start and end apart: 5, of which 5 were waited for; matrix products, arithmetic and copies ran while one was open for 0% of the time, Pallas kernels for 0%

commit v1 on v0

--- a/solution.py
+++ b/solution.py
@@ -18,7 +18,15 @@
     differ = first_hot - second_hot
     mix_share = jax.nn.sigmoid(jnp.sum(gate_logits * differ, axis=1))
     mixing = mix_share[:, None] * first_hot + (1.0 - mix_share)[:, None] * second_hot
-    local_rows = lax.all_to_all(expert_rows, "exp", split_axis=1, concat_axis=0, tiled=True)
+
+    def object_map(row_data):
+        lower = jnp.concatenate(
+            lax.all_to_all(jnp.stack(jnp.split(row_data, lax.psum(1, "exp"), axis=1)), "exp", 0, 0),
+            axis=0,
+        )
+        return lower
+
+    local_rows = object_map(expert_rows)
     local_wide = local_rows.astype(jnp.float32)
     mixed_own = jnp.sum(mixing.T[:, :, None] * local_wide, axis=0).astype(jnp.bfloat16)
     mixed_rows, group_targets = (

time: 543 us -> 512 us (0.943)
  other arithmetic: 28.4 us -> 9.78 us
  local copies, waits for them, and re-layouts: 19.7 us -> 4.12 us
    unnamed x20 -> x14, local copies, waits for them, and re-layouts: 18 us -> 2.33 us
    unnamed x1 -> x0, other arithmetic: 13.5 us -> none
  transfers between devices with their start and end apart: 5 -> 5, of which waited for: 5 -> 5; matrix products, arithmetic and copies ran while one was open for 0% -> 1% of each run, Pallas kernels for 0% -> 0%
where the time goes in v1:
time: 512 us
  waiting for transfers between devices  381 us (74%)
  blocking collectives  59.7 us (12%)
  matrix products  35.5 us (7%)
  between operations  16.3 us (3%)
  other arithmetic  9.78 us (2%)
  starting transfers between devices  5.57 us (1%)
    all_gather x1, waiting for transfers between devices, shards(): full_head = lax.all_gather(head, 'tok', axis=0, tiled=True)  165 us
    psum x1, waiting for transfers between devices, shards(): router_sum = lax.psum(router_part, ('tok', 'exp'))  83 us
    all_to_all x1, waiting for transfers between devices, object_map(): lax.all_to_all(jnp.stack(jnp.split(row_data, lax.psum(1, 'exp'), axis=1))...  47.1 us
    reduce_scatter x1, waiting for transfers between devices, shards(): lax.psum_scatter(lax.dot_general(slope, full_head, (((1,), (1,)), ((), ()...  45.4 us
    psum x1, blocking collectives, shards(): loss_sum = lax.psum(jnp.sum(own_loss), ('tok', 'exp'))  39.4 us
    all_gather x1, waiting for transfers between devices, shards(): lax.all_gather(mixed_own, 'exp', axis=0, tiled=True)  39.1 us
    dot_general x1, matrix products, shards(): lax.dot_general(slope, full_head, (((1,), (1,)), ((), ())), preferred_ele...  17.2 us
    dot_general x1, matrix products, shards(): logits = jnp.dot(mixed_rows, full_head, preferred_element_type=jnp.float32)  16.9 us
  transfers between devices with their start and end apart: 5, of which 5 were waited for; matrix products, arithmetic and copies ran while one was open for 1% of the time, Pallas kernels for 0%

profile of v1, /device:TPU:1, one launch (start us, length us, event | category | flops | bytes accessed | tf_op | source)
XLA Modules:
  0.0 511.5 jit_solution(1747222428845513638)
XLA Ops:
  7.2 0.0 copy-start
  7.2 1.8 slice_bitcast_fusion.3
  9.0 0.0 copy-start.2
  9.0 0.0 copy-start.1
  9.0 1.6 pad_maximum_fusion
  10.6 5.4 %all-to-all-start = ((bf16[4,1,64,4096]{3,2,1,0:T(8,128)(2,1)}), bf16[4,1,64,4096]{3,2,1,0:T(8,128)(2,1)S(1)}, u32[]{:S(2)}, u32[]{:S(2)}) async-start(bf16[4,1,64,4096]{3,2,1,0:T(8,128)(2,1)} %pad_maximum_fusion), calls=%async_computation | async-start | bytes 4194304 | tf_op jit(solution)/shard_map/all_to_all | solution.py:24
  16.0 0.0 copy-start.4
  16.0 0.0 copy-start.3
  16.0 0.0 all-gather.3.cloned.1.call-start
  16.1 0.0 copy-done.2
  16.1 0.0 copy-done
  16.1 0.0 copy-done.1
  16.1 0.5 fusion.11
  16.7 47.1 %all-to-all-done = bf16[4,1,64,4096]{3,2,1,0:T(8,128)(2,1)S(1)} async-done(((bf16[4,1,64,4096]{3,2,1,0:T(8,128)(2,1)}), bf16[4,1,64,4096]{3,2,1,0:T(8,128)(2,1)S(1)}, u32[]{:S(2)}, u32[]{:S(2)}) %all-to-all-start) | async-done | bytes 2097184 | tf_op jit(solution)/shard_map/all_to_all | solution.py:24
  63.8 1.4 fusion
  65.2 0.0 all-gather.3.cloned.1.call-update
  65.2 0.0 all-gather.5.cloned.1.call-start
  65.2 0.7 all-gather.5.cloned.1.call-update
  65.9 0.0 reduce-scatter.2.cloned.1.call-start
  66.0 0.0 copy-done.4
  66.0 0.6 dynamic-slice
  67.3 0.0 copy-done.3
  67.3 0.2 dynamic-update-slice
  67.5 4.0 all-reduce
  71.5 39.1 %all-gather.3.cloned.1.call-done = bf16[256,4096]{1,0:T(8,128)(2,1)} async-done(((bf16[64,4096]{1,0:T(8,128)(2,1)}), bf16[256,4096]{1,0:T(8,128)(2,1)}) %all-gather.3.cloned.1.call-update) | async-done | bytes 2097168 | tf_op jit(solution)/shard_map/all_gather | solution.py:33
  110.7 165.1 %all-gather.5.cloned.1.call-done = bf16[4096,4000]{0,1:T(8,128)(2,1)} async-done(((bf16[512,4000]{0,1:T(8,128)(2,1)}), bf16[4096,4000]{0,1:T(8,128)(2,1)}) %all-gather.5.cloned.1.call-update) | async-done | bytes 32768016 | tf_op jit(solution)/shard_map/all_gather | solution.py:37
  275.8 16.9 %fusion.20 = (f32[256]{0:T(256)S(1)}, f32[256,4000]{0,1:T(8,128)}) fusion(bf16[256,4096]{1,0:T(8,128)(2,1)} %all-gather.3.cloned.1.call-done, bf16[4096,4000]{0,1:T(8,128)(2,1)} %all-gather.5.cloned.1.call-done), kind=kOutput, calls=%fused_computation.46 | convolution fusion | flops 8389632000 | bytes 38962176 | tf_op jit(solution)/shard_map/dot_general | solution.py:38
  292.7 9.6 %pmax.7 = f32[256]{0:T(256)S(1)} all-reduce(f32[256]{0:T(256)S(1)} %get-tuple-element.19), channel_id=1, replica_groups=mesh['tok'=8,'exp'=4] {'exp'}, use_global_device_ids=true, to_apply=%region_3.4 | all-reduce | flops 256 | bytes 2048 | tf_op jit(solution)/shard_map/pmax | solution.py:44
  302.3 3.9 fusion.2
  306.2 6.6 %all-reduce.1 = (f32[256]{0:T(256)S(1)}, f32[256]{0:T(256)S(1)}) all-reduce(f32[256]{0:T(256)S(1)} %get-tuple-element.4, f32[256]{0:T(256)S(1)} %get-tuple-element.3), channel_id=1, replica_groups=mesh['tok'=8,'exp'=4] {'exp'}, use_global_device_ids=true, to_apply=%region_5.6 | all-reduce | flops 512 | bytes 4096 | tf_op jit(solution)/shard_map/psum | solution.py:45
  312.8 17.2 %convolution_convert_fusion = bf16[256,4096]{1,0:T(8,128)(2,1)} fusion(bf16[4096,4000]{0,1:T(8,128)(2,1)} %all-gather.5.cloned.1.call-done, f32[256,4000]{0,1:T(8,128)} %get-tuple-element.20, f32[256]{0:T(256)S(1)} %get-tuple-element.10, s32[256]{0:T(256)S(1)} %all-reduce, s32[4000]{0:T(1024)S(1)} %iota_add_fusion), kind=kOutput, calls=%fused_computation.2 | convolution fusion | flops 8395800576 | bytes 38979200 | tf_op jit(solution)/shard_map/dot_general | solution.py:56
  330.0 0.0 reduce-scatter.2.cloned.1.call-update
  330.0 0.0 all-reduce.4.cloned.1.call-start
  330.1 45.4 %reduce-scatter.2.cloned.1.call-done = bf16[64,4096]{1,0:T(8,128)(2,1)} async-done(((bf16[256,4096]{1,0:T(8,128)(2,1)}), bf16[64,4096]{1,0:T(8,128)(2,1)}) %reduce-scatter.2.cloned.1.call-update) | async-done | bytes 524304 | tf_op jit(solution)/shard_map/reduce_scatter | solution.py:55
  375.4 1.1 convert_element_type.36
  376.5 0.5 fusion.1
  377.1 1.0 convolution_bitcast_fusion
  378.1 0.0 all-reduce.4.cloned.1.call-update
  378.1 1.2 fusion.18
  379.3 39.4 %psum.31 = f32[]{:T(128)} all-reduce(f32[]{:T(128)} %get-tuple-element.7), channel_id=1, replica_groups=mesh['tok'=8,'exp'=4] {'tok','exp'}, use_global_device_ids=true, to_apply=%region_13.14 | all-reduce | flops 1 | bytes 8 | tf_op jit(solution)/shard_map/psum | solution.py:51
  419.3 83.0 %all-reduce.4.cloned.1.call-done = f32[4096,4]{0,1:T(4,128)} async-done(((f32[4096,4]{0,1:T(4,128)}), f32[4096,4]{0,1:T(4,128)}) %all-reduce.4.cloned.1.call-update) | async-done | bytes 65552 | tf_op jit(solution)/shard_map/psum | solution.py:67
  502.4 1.5 copy.11
  (8 shorter events, 0.1 us)
Async XLA Ops:
  7.2 8.9 %copy-start = (bf16[64,4096]{1,0:T(8,128)(2,1)S(1)}, bf16[64,4096]{1,0:T(8,128)(2,1)}, u32[]{:S(2)}) copy-start(bf16[64,4096]{1,0:T(8,128)(2,1)} %param.7) | copy-start | bytes 1572868
  9.0 7.1 %copy-start.2 = (s32[64,2]{0,1:T(2,128)S(1)}, s32[64,2]{0,1:T(2,128)}, u32[]{:S(2)}) copy-start(s32[64,2]{0,1:T(2,128)} %param.9) | copy-start | bytes 1540
  9.0 7.1 %copy-start.1 = (f32[4096,4]{0,1:T(4,128)S(1)}, f32[4096,4]{0,1:T(4,128)}, u32[]{:S(2)}) copy-start(f32[4096,4]{0,1:T(4,128)} %param.8) | copy-start | bytes 196612
  10.6 53.2 %all-to-all-start = ((bf16[4,1,64,4096]{3,2,1,0:T(8,128)(2,1)}), bf16[4,1,64,4096]{3,2,1,0:T(8,128)(2,1)S(1)}, u32[]{:S(2)}, u32[]{:S(2)}) async-start(bf16[4,1,64,4096]{3,2,1,0:T(8,128)(2,1)} %pad_maximum_fusion), calls=%async_computation | async-start | bytes 4194304 | tf_op jit(solution)/shard_map/all_to_all | solution.py:24
  16.0 50.0 %copy-start.4 = (u32[32]{0:T(128)S(1)}, u32[32]{0:T(128)}, u32[]{:S(2)}) copy-start(u32[32]{0:T(128)} %constant.28) | copy-start | bytes 388
  16.0 51.2 %copy-start.3 = (s32[64]{0:T(128)S(1)}, s32[64]{0:T(128)}, u32[]{:S(2)}) copy-start(s32[64]{0:T(128)} %param.10) | copy-start | bytes 772
  16.0 94.6 %all-gather.3.cloned.1.call-start = ((), (), s32[]{:S(2)}) async-start(), calls=%async_computation.2 | async-start | bytes 2621440 | tf_op jit(solution)/shard_map/all_gather | solution.py:33
  65.2 210.6 %all-gather.5.cloned.1.call-start = ((), (), s32[]{:S(2)}) async-start(), calls=%async_computation.3 | async-start | bytes 36864000 | tf_op jit(solution)/shard_map/all_gather | solution.py:37
  65.9 309.5 %reduce-scatter.2.cloned.1.call-start = ((), (), s32[]{:S(2)}) async-start(), calls=%async_computation.4 | async-start | bytes 2621440 | tf_op jit(solution)/shard_map/reduce_scatter | solution.py:55
  330.0 172.4 %all-reduce.4.cloned.1.call-start = ((), (), s32[]{:S(2)}) async-start(), calls=%async_computation.5 | async-start | bytes 131072 | tf_op jit(solution)/shard_map/psum | solution.py:67
Sparse Core Ops, SparseCore 0:
  65.3 45.3 all-gather.2
  112.5 163.2 all-gather.4
  330.1 45.2 reduce-scatter.1
  381.4 120.8 all-reduce.3
